TPU v7x, 32 devices: a whole 2x2x4 slice. The times are simulated.
32 devices in a mesh: seq: 8 (over z, y), head: 4 (over x, core).
Axes of the slice: x: 2, y: 2, z: 4, core: 2. Of those that a mesh axis runs over, the one named last changes fastest.
Arguments:
- q_nope: bfloat16 [4, 64, 128], P(None, 'head'), may hold values from -5 to 5
- q_rope: bfloat16 [4, 64, 64], P(None, 'head'), may hold values from -16 to 16
- w_key_up: bfloat16 [64, 128, 512], P('head'), may hold values from -0.5 to 0.5
- w_value_up: bfloat16 [64, 512, 128], P('head'), may hold values from -0.25 to 0.25
- latent_cache: bfloat16 [512, 64, 576], P('seq'), may hold values from -34 to 34
- page_scale: float32 [512], P('seq'), may hold values from 0.25 to 2, as said below
- block_table: int32 [4, 128], P(None, 'seq'), may hold values from 0 to 63, as said below
- lengths: int32 [4], replicated, may hold values from 1 to 8192, 20480 in all
Outputs:
- attn_out: bfloat16 [4, 8192], P('head', 'seq')
Inputs may be any that keep to these rules, and one draw needn't show every extreme that they name: `block_table`: each entry is the number of a page within its pool; for each index of seq, the entries of its 16 page columns over all requests name every page of its pool exactly once. `page_scale`: every page scale is positive. `lengths`: each request has at least one cached position and at most 8192; the longest has exactly 8192.
All inputs are finite; a program needn't handle non-finite values.
Results may differ from a plain program's by a relative error of at most 0.0095.
Values may be sent and summed in bfloat16 or wider, within the bound.
A program may use at most 64 MiB of HBM per device.

v0:
```python
import jax
import jax.numpy as jnp
from jax import lax
from jax.sharding import PartitionSpec as P

ROPE = 64
NOPE = 128


floor_score = -1e30


def shards(q_nope, q_rope, w_key_up, w_value_up, latent_cache, page_scale, block_table, lengths):
    softmax_scale = (NOPE + ROPE) ** (-0.5)
    batch_rows, window = block_table.shape
    page_len = latent_cache.shape[1]
    ctx_local = window * page_len
    lat_width = latent_cache.shape[2] - q_rope.shape[2]
    value_up = w_value_up.astype(jnp.float32)
    q_latent = jnp.einsum(
        "bhn,hnl->bhl", q_nope, w_key_up, preferred_element_type=jnp.float32
    ).astype(jnp.bfloat16)
    cache_rows = latent_cache[block_table].reshape(batch_rows, ctx_local, latent_cache.shape[2])
    latent_rows = cache_rows[:, :, :lat_width]
    rope_rows = cache_rows[:, :, lat_width:]
    scale_rows = jnp.repeat(page_scale[block_table], page_len, axis=1)
    raw_scores = jnp.einsum(
        "bhl,btl->bht", q_latent, latent_rows, preferred_element_type=jnp.float32
    )
    raw_scores = raw_scores + jnp.einsum(
        "bhr,btr->bht", q_rope, rope_rows, preferred_element_type=jnp.float32
    )
    positions = lax.axis_index("seq") * ctx_local + jnp.arange(ctx_local, dtype=jnp.int32)
    usable = (positions[None, :] < lengths[:, None])[:, None, :]
    scores = jnp.where(usable, raw_scores * (scale_rows * softmax_scale)[:, None, :], floor_score)
    local_peak = jnp.max(scores, axis=2)
    maximum = lax.pmax(local_peak, "seq")
    weights = jnp.where(usable, jnp.exp(scores - maximum[..., None]), 0.0)
    denominator = jnp.sum(weights, axis=2)
    probabilities = (weights * scale_rows[:, None, :]).astype(jnp.bfloat16)
    weighted = jnp.einsum(
        "bht,btl->bhl", probabilities, latent_rows, preferred_element_type=jnp.float32
    )
    carried = jnp.einsum("bhl,hlv->bhv", weighted, value_up, precision=lax.Precision.HIGHEST)
    denominator, carried = (denominator, carried)
    denominator, carried = lax.psum((denominator, carried), "seq")
    projected = carried / denominator[..., None]
    flattened = projected.reshape(batch_rows, projected.shape[1] * projected.shape[2]).astype(
        jnp.bfloat16
    )
    regrouped = lax.all_to_all(flattened, "head", split_axis=0, concat_axis=1, tiled=True)
    column_width = regrouped.shape[1] // lax.axis_size("seq")
    return lax.dynamic_slice_in_dim(
        regrouped, lax.axis_index("seq") * column_width, column_width, 1
    )


def solution(mesh):
    in_specs = (
        P(None, "head", None),
        P(None, "head", None),
        P("head", None, None),
        P("head", None, None),
        P("seq", None, None),
        P("seq"),
        P(None, "seq"),
        P(),
    )
    out_specs = P("head", "seq")
    return jax.shard_map(shards, mesh=mesh, in_specs=in_specs, out_specs=out_specs, check_vma=False)
```

profile of v0, /device:TPU:0, one launch (start us, length us, event | category | flops | bytes accessed | tf_op | source)
XLA Modules:
  0.0 85.4 jit_solution(14951655192551862558)
XLA Ops:
  0.0 0.0 copy-start
  0.0 0.8 compare_select_fusion
  0.8 0.1 reshape.63
  0.9 0.0 copy-start.3
  0.9 0.0 copy-start.2
  1.0 6.0 %gather_fusion = bf16[64,64,576]{2,1,0:T(8,128)(2,1)} fusion(bf16[64,64,576]{2,1,0:T(8,128)(2,1)} %param.12, s32[1024]{0:T(1024)S(1)} %pad_clamp_fusion), kind=kCustom, calls=%fused_computation | custom fusion | bytes 9437440 | tf_op jit(solution)/shard_map/gather | solution.py:23
  6.9 0.0 copy-done.1
  6.9 0.8 gather_fusion.1
  7.7 0.1 reshape.70
  7.8 0.1 broadcast_in_dim.33
  7.9 0.1 reshape.60
  8.0 0.0 copy-done.3
  8.0 0.1 broadcast_compare_fusion
  8.1 0.0 copy-done
  8.1 0.0 copy-done.2
  8.1 0.4 fusion.7
  8.5 3.4 %fusion.2 = f32[4,16,1024]{2,1,0:T(8,128)S(1)} fusion(bf16[4,1024,576]{2,1,0:T(8,128)(2,1)} %bitcast.19, bf16[4,16,512]{2,0,1:T(4,128)(2,1)S(1)} %fusion.7), kind=kOutput, calls=%fused_computation.4 | convolution fusion | flops 67108864 | bytes 4521984 | tf_op jit(solution)/shard_map/bhl,btl->bht/dot_general | solution.py:27
  11.8 0.0 copy-done.4
  11.8 1.7 %fusion.19 = (f32[4,16]{1,0:T(4,128)S(1)}, f32[4,16,1024]{2,1,0:T(8,128)S(1)}) fusion(f32[4,1024]{1,0:T(4,128)S(1)} %broadcast_multiply_fusion, f32[4,16,1024]{2,1,0:T(8,128)S(1)} %fusion.2, bf16[4,16,64]{2,1,0:T(8,128)(2,1)S(1)} %copy-done.4, bf16[4,1024,576]{2,1,0:T(8,128)(2,1)} %bitcast.20, pred[4,1024]{1,0:T(4,128)(4,1)S(1)} %broadcast_compare_fusion), kind=kOutput, calls=%fused_computation.33 | convolution fusion | flops 8650688 | bytes 1601792 | tf_op jit(solution)/shard_map/bhr,btr->bht/dot_general | solution.py:30
  13.6 23.2 %pmax.7 = f32[4,16]{1,0:T(4,128)S(1)} all-reduce(f32[4,16]{1,0:T(4,128)S(1)} %get-tuple-element.7), channel_id=1, replica_groups=mesh['seq'=8,'head'=4] {'seq'}, use_global_device_ids=true, to_apply=%region_1.2 | all-reduce | flops 64 | bytes 512 | tf_op jit(solution)/shard_map/pmax | solution.py:37
  36.7 2.9 %fusion = f32[4,16,512]{2,1,0:T(8,128)S(1)} fusion(bf16[4,1024,576]{2,1,0:T(8,128)(2,1)} %bitcast.21, f32[4,16,1024]{2,1,0:T(8,128)S(1)} %get-tuple-element.8, f32[4,1024]{1,0:T(4,128)S(1)} %reshape.60, f32[4,16]{1,0:T(4,128)S(1)} %pmax.7, pred[4,1024]{1,0:T(4,128)(4,1)S(1)} %broadcast_compare_fusion), kind=kOutput, calls=%fused_computation.2 | convolution fusion | flops 67371008 | bytes 4608256 | tf_op jit(solution)/shard_map/bht,btl->bhl/dot_general | solution.py:41
  39.6 0.2 fusion.9
  39.8 2.6 %convolution_bitcast_fusion.1 = f32[4,16,128]{2,0,1:T(4,128)S(1)} fusion(bf16[16,512,128]{2,1,0:T(8,128)(2,1)} %param.11, f32[4,16,512]{2,1,0:T(8,128)S(1)} %fusion), kind=kOutput, calls=%fused_computation.12 | convolution fusion | flops 50331648 | bytes 2260992 | tf_op jit(solution)/shard_map/bhl,hlv->bhv/dot_general | solution.py:44
  42.4 33.3 %all-reduce = (f32[4,16,128]{2,0,1:T(4,128)S(1)}, f32[4,16]{1,0:T(4,128)S(1)}) all-reduce(f32[4,16,128]{2,0,1:T(4,128)S(1)} %convolution_bitcast_fusion.1, f32[4,16]{1,0:T(4,128)S(1)} %fusion.9), channel_id=1, replica_groups=mesh['seq'=8,'head'=4] {'seq'}, use_global_device_ids=true, to_apply=%region_2.3 | all-reduce | flops 8256 | bytes 66048 | tf_op jit(solution)/shard_map/psum | solution.py:46
  75.7 0.1 copy.20
  75.8 0.1 fusion.17
  75.9 0.5 broadcast.41
  76.4 0.7 reduce
  77.1 0.6 reshape.82
  77.7 3.2 %all-to-all-start = ((bf16[4,2,1024]{2,1,0:T(2,128)(2,1)}), bf16[4,2,1024]{2,1,0:T(2,128)(2,1)S(1)}, u32[]{:S(2)}, u32[]{:S(2)}) async-start(bf16[4,2,1024]{2,1,0:T(2,128)(2,1)} %reshape.82), calls=%async_computation | async-start | bytes 32768 | tf_op jit(solution)/shard_map/all_to_all | solution.py:51
  81.0 3.8 %all-to-all-done = bf16[4,2,1024]{2,1,0:T(2,128)(2,1)S(1)} async-done(((bf16[4,2,1024]{2,1,0:T(2,128)(2,1)}), bf16[4,2,1024]{2,1,0:T(2,128)(2,1)S(1)}, u32[]{:S(2)}, u32[]{:S(2)}) %all-to-all-start) | async-done | bytes 16416 | tf_op jit(solution)/shard_map/all_to_all | solution.py:51
  84.8 0.6 constant_dynamic-slice_fusion
  (6 shorter events, 0.0 us)
Async XLA Ops:
  0.0 8.1 %copy-start = (bf16[16,128,512]{2,1,0:T(8,128)(2,1)S(1)}, bf16[16,128,512]{2,1,0:T(8,128)(2,1)}, u32[]{:S(2)}) copy-start(bf16[16,128,512]{2,1,0:T(8,128)(2,1)} %param.10) | copy-start | bytes 6291460
  0.9 6.0 %copy-start.1 = (f32[64]{0:T(128)S(1)}, f32[64]{0:T(128)}, u32[]{:S(2)}) copy-start(f32[64]{0:T(128)} %param.13) | copy-start | bytes 772
  0.9 7.0 %copy-start.3 = (s32[4]{0:T(128)S(1)}, s32[4]{0:T(128)}, u32[]{:S(2)}) copy-start(s32[4]{0:T(128)} %param.15) | copy-start | bytes 52
  0.9 7.1 %copy-start.2 = (bf16[4,16,128]{2,1,0:T(8,128)(2,1)S(1)}, bf16[4,16,128]{2,1,0:T(8,128)(2,1)}, u32[]{:S(2)}) copy-start(bf16[4,16,128]{2,1,0:T(8,128)(2,1)} %param.8) | copy-start | bytes 49156
  6.9 4.9 %copy-start.4 = (bf16[4,16,64]{2,1,0:T(8,128)(2,1)S(1)}, bf16[4,16,64]{2,1,0:T(8,128)(2,1)}, u32[]{:S(2)}) copy-start(bf16[4,16,64]{2,1,0:T(8,128)(2,1)} %param.9) | copy-start | bytes 24580
  77.7 7.1 %all-to-all-start = ((bf16[4,2,1024]{2,1,0:T(2,128)(2,1)}), bf16[4,2,1024]{2,1,0:T(2,128)(2,1)S(1)}, u32[]{:S(2)}, u32[]{:S(2)}) async-start(bf16[4,2,1024]{2,1,0:T(2,128)(2,1)} %reshape.82), calls=%async_computation | async-start | bytes 32768 | tf_op jit(solution)/shard_map/all_to_all | solution.py:51
where the time goes:
time: 85.8 us; the launch traced here: 85.4 us
  blocking collectives  56.5 us (66%)
  matrix products  11 us (13%)
  local copies, waits for them, and re-layouts  8.95 us (10%)
  waiting for transfers between devices  3.82 us (4%)
  starting transfers between devices  3.25 us (4%)
  other arithmetic  1.89 us (2%)
    psum x1, blocking collectives, shards(): denominator, carried = lax.psum((denominator, carried), 'seq')  33.3 us
    pmax x1, blocking collectives, shards(): maximum = lax.pmax(local_peak, 'seq')  23.2 us
    gather x1, local copies, waits for them, and re-layouts, shards(): latent_cache[block_table]  5.98 us
    all_to_all x1, waiting for transfers between devices, shards(): lax.all_to_all(flattened, 'head', split_axis=0, concat_axis=1, tiled=True)  3.82 us
    dot_general x1, matrix products, shards(): jnp.einsum('bhl,btl->bht', q_latent, latent_rows, preferred_element_type=...  3.39 us
    all_to_all x1, starting transfers between devices, shards(): lax.all_to_all(flattened, 'head', split_axis=0, concat_axis=1, tiled=True)  3.25 us
    dot_general x1, matrix products, shards(): jnp.einsum('bht,btl->bhl', probabilities, latent_rows, preferred_element_...  2.89 us
    dot_general x1, matrix products, shards(): jnp.einsum('bhl,hlv->bhv', weighted, value_up, precision=lax.Precision.HI...  2.59 us
  transfers between devices with their start and end apart: 1, of which 1 were waited for; matrix products, arithmetic and copies ran while one was open for 0% of the time, Pallas kernels for 0%

commit v1 on v0

v1 whole, which is shorter than its diff:
```python
import functools

import jax
import jax.numpy as jnp
from jax import lax
from jax.experimental import pallas as pl
from jax.experimental.pallas import tpu as pltpu
from jax.sharding import PartitionSpec as P

floor_score = -1e30
floor_peak = -1e29
LANES = 128
CHUNKS = 4
WK_PARTS = 4
MESH = pl.DeviceIdType.MESH


def loop(count, body):
    if count <= 16:
        for i in range(count):
            body(i)
    else:
        def step(i, carry):
            body(i)
            return carry
        lax.fori_loop(0, count, step, 0)


def kernel(
    n_seq, n_head, width,
    qn_hbm, qr_hbm, wk_hbm, wv_hbm, kv_hbm, scale_hbm, table_hbm, len_ref,
    out_ref,
    qn, qr, wk, wv, kv, scale, table,
    msg, stat, acc_in, stat_in, mix,
    small_sem, wk_sem, kv_sem, wv_sem, send_sem, recv_sem,
):
    batch, heads, nope = qn.shape
    rope = qr.shape[2]
    lat, vdim = wv.shape[1], wv.shape[2]
    pages, page_len, _ = kv.shape
    window = table.shape[1]
    rows = batch * heads
    per_msg = msg.shape[1]
    per_shard = n_seq // n_head
    softmax_scale = (nope + rope) ** (-0.5)
    my_seq = lax.axis_index("seq")
    my_head = lax.axis_index("head")

    small = [
        pltpu.make_async_copy(src, dst, small_sem.at[i])
        for i, (src, dst) in enumerate(
            ((qn_hbm, qn), (qr_hbm, qr), (scale_hbm, scale), (table_hbm, table))
        )
    ]
    for copy in small:
        copy.start()
    wk_step = heads // WK_PARTS
    wk_copies = [
        pltpu.make_async_copy(
            wk_hbm.at[pl.ds(i * wk_step, wk_step)], wk.at[pl.ds(i * wk_step, wk_step)], wk_sem.at[i]
        )
        for i in range(WK_PARTS)
    ]
    for copy in wk_copies:
        copy.start()
    kv_step = pages // CHUNKS
    kv_copies = [
        pltpu.make_async_copy(
            kv_hbm.at[pl.ds(i * kv_step, kv_step)], kv.at[pl.ds(i * kv_step, kv_step)], kv_sem.at[i]
        )
        for i in range(CHUNKS)
    ]
    for copy in kv_copies:
        copy.start()
    wv_copy = pltpu.make_async_copy(wv_hbm, wv, wv_sem.at[0])
    wv_copy.start()

    barrier = pltpu.get_barrier_semaphore()
    source_head = my_seq // per_shard
    own = source_head == my_head

    def greet(i):
        @pl.when(jnp.logical_not(jnp.logical_and(own, i == my_seq)))
        def _():
            pl.semaphore_signal(
                barrier, inc=1, device_id=(jnp.int32(i), source_head), device_id_type=MESH
            )

    loop(n_seq, greet)

    for copy in small:
        copy.wait()

    lane = lax.broadcasted_iota(jnp.int32, (batch, LANES), 1)
    request = lax.broadcasted_iota(jnp.int32, (batch, LANES), 0)
    length = jnp.zeros((batch, LANES), jnp.int32)
    for b in range(batch):
        length = jnp.where(request == b, len_ref[b], length)
    base = my_seq * (window * page_len)
    names = table[...]
    counts = jnp.zeros((batch, LANES), jnp.float32)
    for j in range(window):
        held = jnp.clip(length - (base + j * page_len), 0, page_len).astype(jnp.float32)
        counts = jnp.where(names[:, j : j + 1] == lane, held, counts)
    s_row = scale[...]
    s_hi = s_row.astype(jnp.bfloat16)
    s_rest = s_row - s_hi.astype(jnp.float32)
    s_mid = s_rest.astype(jnp.bfloat16)
    s_low = (s_rest - s_mid.astype(jnp.float32)).astype(jnp.bfloat16)
    per_page = jnp.concatenate(
        [counts[:, :pages]]
        + [s.astype(jnp.float32) for s in (s_hi, s_mid, s_low)]
        + [jnp.zeros((1, pages), jnp.float32)] * (8 - batch - 3),
        axis=0,
    ).astype(jnp.bfloat16)
    positions = pages * page_len
    spread = (
        lax.broadcasted_iota(jnp.int32, (pages, positions), 1) // page_len
        == lax.broadcasted_iota(jnp.int32, (pages, positions), 0)
    ).astype(jnp.float32).astype(jnp.bfloat16)
    per_pos = jnp.dot(per_page, spread, preferred_element_type=jnp.float32)
    scale_pos = per_pos[batch : batch + 1] + per_pos[batch + 1 : batch + 2] + per_pos[batch + 2 : batch + 3]

    query = qn[...].reshape(rows, nope).astype(jnp.float32)
    row_head = lax.broadcasted_iota(jnp.int32, (rows, nope), 0) % heads
    q_lat = jnp.zeros((rows, lat), jnp.float32)
    for i in range(WK_PARTS):
        wide = jnp.concatenate(
            [jnp.where(row_head == h, query, 0.0) for h in range(i * wk_step, (i + 1) * wk_step)],
            axis=1,
        ).astype(jnp.bfloat16)
        wk_copies[i].wait()
        block = wk[pl.ds(i * wk_step, wk_step)].reshape(wk_step * nope, lat)
        q_lat = q_lat + jnp.dot(wide, block, preferred_element_type=jnp.float32)
    q_all = jnp.concatenate([q_lat.astype(jnp.bfloat16), qr[...].reshape(rows, rope)], axis=1)

    span = kv_step * page_len
    offset = (lax.broadcasted_iota(jnp.int32, (1, span), 1) % page_len).astype(jnp.float32)
    parts = []
    for c in range(CHUNKS):
        kv_copies[c].wait()
        block = kv[pl.ds(c * kv_step, kv_step)].reshape(span, lat + rope)
        raw = lax.dot_general(
            q_all, block, (((1,), (1,)), ((), ())), preferred_element_type=jnp.float32
        )
        s_pos = scale_pos[:, c * span : (c + 1) * span]
        score = raw * (s_pos * softmax_scale)
        score = jnp.concatenate(
            [
                jnp.where(
                    jnp.broadcast_to(offset, (heads, span))
                    < jnp.broadcast_to(per_pos[b : b + 1, c * span : (c + 1) * span], (heads, span)),
                    score[b * heads : (b + 1) * heads],
                    floor_score,
                )
                for b in range(batch)
            ],
            axis=0,
        )
        peak = jnp.maximum(jnp.max(score, axis=1, keepdims=True), floor_peak)
        weight = jnp.exp(score - peak)
        total = jnp.sum(weight, axis=1, keepdims=True)
        prob = (weight * s_pos).astype(jnp.bfloat16)
        acc = jnp.dot(prob, block[:, :lat], preferred_element_type=jnp.float32)
        parts.append((peak, total, acc))
    peak = functools.reduce(jnp.maximum, [p[0] for p in parts])
    total = jnp.zeros((rows, 1), jnp.float32)
    acc = jnp.zeros((rows, lat), jnp.float32)
    for p, t, a in parts:
        factor = jnp.exp(p - peak)
        total = total + t * factor
        acc = acc + a * factor

    col = lax.broadcasted_iota(jnp.int32, (rows, LANES), 1)
    pair = jnp.where(col == 0, peak, jnp.where(col == 1, total, 0.0))
    pair = jnp.concatenate([pair, jnp.zeros((LANES - rows, LANES), jnp.float32)], axis=0)
    stat[...] = pair.T[0:2]

    high = acc.astype(jnp.bfloat16)
    low = (acc - high.astype(jnp.float32)).astype(jnp.bfloat16)
    both = jnp.concatenate([high, low], axis=0)
    out_head = lax.broadcasted_iota(jnp.int32, (rows, vdim), 0) % heads
    carried = jnp.zeros((rows, vdim), jnp.float32)
    wv_copy.wait()
    for h in range(0, heads, 2):
        y = jnp.dot(
            both, jnp.concatenate([wv[h], wv[h + 1]], axis=1), preferred_element_type=jnp.float32
        )
        y = y[:rows] + y[rows:]
        carried = jnp.where(out_head == h, y[:, :vdim], carried)
        carried = jnp.where(out_head == h + 1, y[:, vdim:], carried)
    msg[...] = carried.reshape(msg.shape)

    n_dest = per_shard * n_head

    @pl.when(own)
    def _():
        pl.semaphore_wait(barrier, n_dest - 1)

    @pl.when(jnp.logical_not(own))
    def _():
        pl.semaphore_wait(barrier, n_dest)

    def target(k):
        part, request_of = k // n_head, k % n_head
        slot = request_of * (heads // per_msg) + (part * width) // (vdim * per_msg)
        return my_head * per_shard + part, request_of, slot

    def pair_to(k):
        seq_of, head_of, slot = target(k)
        return [
            pltpu.make_async_remote_copy(
                src_ref=src, dst_ref=dst, send_sem=send_sem.at[n, k], recv_sem=recv_sem.at[n, my_seq],
                device_id=(jnp.int32(seq_of), jnp.int32(head_of)), device_id_type=MESH,
            )
            for n, (src, dst) in enumerate(
                ((stat, stat_in.at[my_seq]), (msg.at[slot], acc_in.at[my_seq]))
            )
        ]

    def local_pair(k):
        slot = target(k)[2]
        return [
            pltpu.make_async_copy(src, dst, recv_sem.at[n, my_seq])
            for n, (src, dst) in enumerate(
                ((stat, stat_in.at[my_seq]), (msg.at[slot], acc_in.at[my_seq]))
            )
        ]

    def is_me(k):
        seq_of, head_of, _ = target(k)
        return jnp.logical_and(seq_of == my_seq, head_of == my_head)

    def send(k):
        @pl.when(jnp.logical_not(is_me(k)))
        def _():
            for copy in pair_to(k):
                copy.start()

        @pl.when(is_me(k))
        def _():
            for copy in local_pair(k):
                copy.start()

    loop(n_dest, send)

    def receive(i):
        for n, (src, dst) in enumerate(((stat, stat_in.at[i]), (msg.at[0], acc_in.at[i]))):
            pltpu.make_async_copy(src, dst, recv_sem.at[n, i]).wait()

    loop(n_seq, receive)

    peaks, totals = stat_in[:, 0, :], stat_in[:, 1, :]
    factor = jnp.exp(peaks - jnp.max(peaks, axis=0, keepdims=True))
    denominator = jnp.sum(factor * totals, axis=0, keepdims=True)
    used = lax.broadcasted_iota(jnp.int32, (1, LANES), 1) < rows
    factor = factor / jnp.where(used, denominator, 1.0)
    if n_seq < LANES:
        factor = jnp.concatenate(
            [factor, jnp.zeros((LANES - n_seq, LANES), jnp.float32)], axis=0
        )
    mix[...] = factor.T.reshape(mix.shape)
    first = (my_seq % per_shard) * width
    weights = mix[my_head * (heads // per_msg) + first // (vdim * per_msg)]
    result = jnp.zeros((per_msg, vdim), jnp.float32)
    for i in range(n_seq):
        result = result + weights[:, i : i + 1] * acc_in[i]
    if width >= vdim:
        for r in range(per_msg):
            out_ref[:, r * vdim : (r + 1) * vdim] = result[r : r + 1].astype(out_ref.dtype)
    else:
        picked = result[:, :width]
        for k in range(1, vdim // width):
            here = (my_seq % (vdim // width)) == k
            picked = jnp.where(here, result[:, k * width : (k + 1) * width], picked)
        out_ref[...] = picked.astype(out_ref.dtype)

    def sent(k):
        @pl.when(jnp.logical_not(is_me(k)))
        def _():
            for copy in pair_to(k):
                copy.wait_send()

    loop(n_dest, sent)


def solution(mesh):
    n_seq, n_head = mesh.shape["seq"], mesh.shape["head"]

    def shards(q_nope, q_rope, w_key_up, w_value_up, latent_cache, page_scale, block_table, lengths):
        batch, heads, _ = q_nope.shape
        vdim = w_value_up.shape[2]
        width = heads * n_head * vdim // n_seq
        per_msg = max(1, width // vdim)
        n_dest = (n_seq // n_head) * n_head
        assert batch == n_head and batch * heads <= LANES and n_seq % n_head == 0
        vmem = lambda a: pltpu.VMEM(a.shape, a.dtype)
        scale_row = page_scale.reshape(1, page_scale.shape[0])
        big = (q_nope, q_rope, w_key_up, w_value_up, latent_cache, scale_row, block_table)
        return pl.pallas_call(
            functools.partial(kernel, n_seq, n_head, width),
            out_shape=jax.ShapeDtypeStruct((1, width), jnp.bfloat16),
            in_specs=[pl.BlockSpec(memory_space=pl.ANY)] * 7
            + [pl.BlockSpec(memory_space=pltpu.SMEM)],
            out_specs=pl.BlockSpec(memory_space=pltpu.VMEM),
            scratch_shapes=[vmem(a) for a in big]
            + [
                pltpu.VMEM((batch * heads // per_msg, per_msg, vdim), jnp.float32),
                pltpu.VMEM((2, LANES), jnp.float32),
                pltpu.VMEM((n_seq, per_msg, vdim), jnp.float32),
                pltpu.VMEM((n_seq, 2, LANES), jnp.float32),
                pltpu.VMEM((LANES // per_msg, per_msg, LANES), jnp.float32),
                pltpu.SemaphoreType.DMA((4,)),
                pltpu.SemaphoreType.DMA((WK_PARTS,)),
                pltpu.SemaphoreType.DMA((CHUNKS,)),
                pltpu.SemaphoreType.DMA((1,)),
                pltpu.SemaphoreType.DMA((2, n_dest)),
                pltpu.SemaphoreType.DMA((2, n_seq)),
            ],
            compiler_params=pltpu.CompilerParams(collective_id=0, has_side_effects=True),
        )(*big, lengths)

    in_specs = (
        P(None, "head", None),
        P(None, "head", None),
        P("head", None, None),
        P("head", None, None),
        P("seq", None, None),
        P("seq"),
        P(None, "seq"),
        P(),
    )
    out_specs = P("head", "seq")
    return jax.shard_map(shards, mesh=mesh, in_specs=in_specs, out_specs=out_specs, check_vma=False)
```

time: 85.8 us -> 18.3 us (0.21)
  blocking collectives: 56.5 us -> 0 us
  Pallas kernels: 0 us -> 16.7 us
  matrix products: 11 us -> 0 us
  local copies, waits for them, and re-layouts: 8.95 us -> 1.28 us
  waiting for transfers between devices: 3.82 us -> 0 us
  starting transfers between devices: 3.25 us -> 0 us
  other arithmetic: 1.89 us -> 0 us
    psum x1 -> x0, blocking collectives: 33.3 us -> none  [shards(): denominator, carried = lax.psum((denominator, carried), 'seq')]
    pmax x1 -> x0, blocking collectives: 23.2 us -> none  [shards(): maximum = lax.pmax(local_peak, 'seq')]
    pallas_call x0 -> x1, Pallas kernels: none -> 16.7 us  [shards(): pl.pallas_call(functools.partial(kernel, n_seq, n_head, width), out_shape...]
    dot_general x5 -> x0, matrix products: 11 us -> none  [the longest x1 3.39 us: shards(): jnp.einsum('bhl,btl->bht', q_latent, latent_rows, preferred_element_type=...]
    gather x3 -> x0, local copies, waits for them, and re-layouts: 6.84 us -> none  [the longest x1 5.98 us: shards(): latent_cache[block_table]]
    all_to_all x1 -> x0, waiting for transfers between devices: 3.82 us -> none  [shards(): lax.all_to_all(flattened, 'head', split_axis=0, concat_axis=1, tiled=True)]
    all_to_all x1 -> x0, starting transfers between devices: 3.25 us -> none  [shards(): lax.all_to_all(flattened, 'head', split_axis=0, concat_axis=1, tiled=True)]
  transfers between devices with their start and end apart: 1 -> 0, of which waited for: 1 -> 0; matrix products, arithmetic and copies ran while one was open for 0% -> 0% of each run, Pallas kernels for 0% -> 0%
where the time goes in v1:
time: 18.3 us; the launch traced here: 18 us
  Pallas kernels  16.7 us (91%)
  local copies, waits for them, and re-layouts  1.28 us (7%)
    pallas_call x1, Pallas kernels, shards(): pl.pallas_call(functools.partial(kernel, n_seq, n_head, width), out_shape...  16.7 us
    unnamed x1, local copies, waits for them, and re-layouts  1.28 us

profile of v1, /device:TPU:0, one launch (start us, length us, event | category | flops | bytes accessed | tf_op | source)
XLA Modules:
  0.0 18.0 jit_solution(6808130334865884860)
XLA Ops:
  0.0 16.7 %shard_map.82 = bf16[1,1024]{1,0:T(2,128)(2,1)} custom-call(bf16[4,16,128]{2,1,0:T(8,128)(2,1)} %qn_hbm.1, bf16[4,16,64]{2,1,0:T(8,128)(2,1)} %qr_hbm.1, bf16[16,128,512]{2,1,0:T(8,128)(2,1)} %wk_hbm.1, bf16[16,512,128]{2,1,0:T(8,128)(2,1)} %wv_hbm.1, bf16[64,64,576]{2,1,0:T(8,128)(2,1)} %kv_hbm.1, f32[1,64]{1,0:T(1,128)} %bitcast.1, s32[4,16]{1,0:T(4,128)} %table_hbm.1, ...), custom_call_target="tpu_custom_call" | custom-call | tf_op jit(solution)/shard_map/pallas_call | solution.py:300
  16.7 1.3 %copy.10 = bf16[1,1024]{1,0:T(2,128)(2,1)} copy(bf16[1,1024]{1,0:T(2,128)(2,1)} %shard_map.82) | data formatting | bytes 4096

commit v2 on v1

--- a/solution.py
+++ b/solution.py
@@ -11,6 +11,8 @@
 floor_peak = -1e29
 LANES = 128
 CHUNKS = 4
+WV_PARTS = 2
+WINDOW = 6
 WK_PARTS = 4
 MESH = pl.DeviceIdType.MESH
 
@@ -54,26 +56,23 @@
     ]
     for copy in small:
         copy.start()
-    wk_step = heads // WK_PARTS
-    wk_copies = [
-        pltpu.make_async_copy(
-            wk_hbm.at[pl.ds(i * wk_step, wk_step)], wk.at[pl.ds(i * wk_step, wk_step)], wk_sem.at[i]
-        )
-        for i in range(WK_PARTS)
-    ]
-    for copy in wk_copies:
-        copy.start()
-    kv_step = pages // CHUNKS
-    kv_copies = [
-        pltpu.make_async_copy(
-            kv_hbm.at[pl.ds(i * kv_step, kv_step)], kv.at[pl.ds(i * kv_step, kv_step)], kv_sem.at[i]
-        )
-        for i in range(CHUNKS)
-    ]
-    for copy in kv_copies:
-        copy.start()
-    wv_copy = pltpu.make_async_copy(wv_hbm, wv, wv_sem.at[0])
-    wv_copy.start()
+    wk_step, kv_step, wv_step = heads // WK_PARTS, pages // CHUNKS, heads // WV_PARTS
+
+    def piece(src, dst, sem, i, step):
+        part = pl.ds(i * step, step)
+        return pltpu.make_async_copy(src.at[part], dst.at[part], sem.at[i])
+
+    wk_copies = [piece(wk_hbm, wk, wk_sem, i, wk_step) for i in range(WK_PARTS)]
+    kv_copies = [piece(kv_hbm, kv, kv_sem, i, kv_step) for i in range(CHUNKS)]
+    wv_copies = [piece(wv_hbm, wv, wv_sem, i, wv_step) for i in range(WV_PARTS)]
+    waiting = wk_copies + kv_copies + wv_copies
+    for _ in range(WINDOW):
+        waiting.pop(0).start()
+
+    def arrive(copy):
+        copy.wait()
+        if waiting:
+            waiting.pop(0).start()
 
     barrier = pltpu.get_barrier_semaphore()
     source_head = my_seq // per_shard
@@ -129,20 +128,21 @@
             [jnp.where(row_head == h, query, 0.0) for h in range(i * wk_step, (i + 1) * wk_step)],
             axis=1,
         ).astype(jnp.bfloat16)
-        wk_copies[i].wait()
+        arrive(wk_copies[i])
         block = wk[pl.ds(i * wk_step, wk_step)].reshape(wk_step * nope, lat)
         q_lat = q_lat + jnp.dot(wide, block, preferred_element_type=jnp.float32)
     q_all = jnp.concatenate([q_lat.astype(jnp.bfloat16), qr[...].reshape(rows, rope)], axis=1)
 
     span = kv_step * page_len
     offset = (lax.broadcasted_iota(jnp.int32, (1, span), 1) % page_len).astype(jnp.float32)
-    parts = []
-    for c in range(CHUNKS):
-        kv_copies[c].wait()
+    def scores(c):
+        arrive(kv_copies[c])
         block = kv[pl.ds(c * kv_step, kv_step)].reshape(span, lat + rope)
-        raw = lax.dot_general(
+        return lax.dot_general(
             q_all, block, (((1,), (1,)), ((), ())), preferred_element_type=jnp.float32
         )
+
+    def attend(c, raw):
         s_pos = scale_pos[:, c * span : (c + 1) * span]
         score = raw * (s_pos * softmax_scale)
         score = jnp.concatenate(
@@ -161,8 +161,17 @@
         weight = jnp.exp(score - peak)
         total = jnp.sum(weight, axis=1, keepdims=True)
         prob = (weight * s_pos).astype(jnp.bfloat16)
-        acc = jnp.dot(prob, block[:, :lat], preferred_element_type=jnp.float32)
-        parts.append((peak, total, acc))
+        values = kv[pl.ds(c * kv_step, kv_step), :, :lat].reshape(span, lat)
+        acc = jnp.dot(prob, values, preferred_element_type=jnp.float32)
+        return peak, total, acc
+
+    parts = []
+    raw = scores(0)
+    for c in range(1, CHUNKS):
+        following = scores(c)
+        parts.append(attend(c - 1, raw))
+        raw = following
+    parts.append(attend(CHUNKS - 1, raw))
     peak = functools.reduce(jnp.maximum, [p[0] for p in parts])
     total = jnp.zeros((rows, 1), jnp.float32)
     acc = jnp.zeros((rows, lat), jnp.float32)
@@ -181,8 +190,9 @@
     both = jnp.concatenate([high, low], axis=0)
     out_head = lax.broadcasted_iota(jnp.int32, (rows, vdim), 0) % heads
     carried = jnp.zeros((rows, vdim), jnp.float32)
-    wv_copy.wait()
     for h in range(0, heads, 2):
+        if h % wv_step == 0:
+            arrive(wv_copies[h // wv_step])
         y = jnp.dot(
             both, jnp.concatenate([wv[h], wv[h + 1]], axis=1), preferred_element_type=jnp.float32
         )
@@ -299,7 +309,7 @@
         big = (q_nope, q_rope, w_key_up, w_value_up, latent_cache, scale_row, block_table)
         return pl.pallas_call(
             functools.partial(kernel, n_seq, n_head, width),
-            out_shape=jax.ShapeDtypeStruct((1, width), jnp.bfloat16),
+            out_shape=pltpu.VMEM((1, width), jnp.bfloat16),
             in_specs=[pl.BlockSpec(memory_space=pl.ANY)] * 7
             + [pl.BlockSpec(memory_space=pltpu.SMEM)],
             out_specs=pl.BlockSpec(memory_space=pltpu.VMEM),
@@ -313,7 +323,7 @@
                 pltpu.SemaphoreType.DMA((4,)),
                 pltpu.SemaphoreType.DMA((WK_PARTS,)),
                 pltpu.SemaphoreType.DMA((CHUNKS,)),
-                pltpu.SemaphoreType.DMA((1,)),
+                pltpu.SemaphoreType.DMA((WV_PARTS,)),
                 pltpu.SemaphoreType.DMA((2, n_dest)),
                 pltpu.SemaphoreType.DMA((2, n_seq)),
             ],

time: 18.3 us -> 15.7 us (0.86)
  Pallas kernels: 16.7 us -> 14.9 us
  local copies, waits for them, and re-layouts: 1.28 us -> 0.6 us
    pallas_call x1, Pallas kernels: 16.7 us -> 14.9 us  [shards(): pl.pallas_call(functools.partial(kernel, n_seq, n_head, width), out_shape...]
    unnamed x1, local copies, waits for them, and re-layouts: 1.28 us -> 0.6 us
where the time goes in v2:
time: 15.7 us; the launch traced here: 15.5 us
  Pallas kernels  14.9 us (95%)
  local copies, waits for them, and re-layouts  0.6 us (4%)
    pallas_call x1, Pallas kernels, shards(): pl.pallas_call(functools.partial(kernel, n_seq, n_head, width), out_shape...  14.9 us
    unnamed x1, local copies, waits for them, and re-layouts  0.6 us

profile of v2, /device:TPU:0, one launch (start us, length us, event | category | flops | bytes accessed | tf_op | source)
XLA Modules:
  0.0 15.5 jit_solution(9726504185985970564)
XLA Ops:
  0.0 14.9 %shard_map.82 = bf16[1,1024]{1,0:T(2,128)(2,1)S(1)} custom-call(bf16[4,16,128]{2,1,0:T(8,128)(2,1)} %qn_hbm.1, bf16[4,16,64]{2,1,0:T(8,128)(2,1)} %qr_hbm.1, bf16[16,128,512]{2,1,0:T(8,128)(2,1)} %wk_hbm.1, bf16[16,512,128]{2,1,0:T(8,128)(2,1)} %wv_hbm.1, bf16[64,64,576]{2,1,0:T(8,128)(2,1)} %kv_hbm.1, f32[1,64]{1,0:T(1,128)} %bitcast.1, s32[4,16]{1,0:T(4,128)} %table_hbm.1, ...), custom_call_target="tpu_custom_call" | custom-call | tf_op jit(solution)/shard_map/pallas_call | solution.py:310
  14.9 0.6 %copy.10 = bf16[1,1024]{1,0:T(2,128)(2,1)} copy(bf16[1,1024]{1,0:T(2,128)(2,1)S(1)} %shard_map.82) | data formatting | bytes 4096

commit v3 on v2

--- a/solution.py
+++ b/solution.py
@@ -30,9 +30,9 @@
 
 def kernel(
     n_seq, n_head, width,
-    qn_hbm, qr_hbm, wk_hbm, wv_hbm, kv_hbm, scale_hbm, table_hbm, len_ref,
+    qn_hbm, qr_hbm, wk_hbm, wv_hbm, kv_hbm, scale_hbm, table_hbm, len_hbm,
     out_ref,
-    qn, qr, wk, wv, kv, scale, table,
+    qn, qr, wk, wv, kv, scale, table, len_ref,
     msg, stat, acc_in, stat_in, mix,
     small_sem, wk_sem, kv_sem, wv_sem, send_sem, recv_sem,
 ):
@@ -51,7 +51,7 @@
     small = [
         pltpu.make_async_copy(src, dst, small_sem.at[i])
         for i, (src, dst) in enumerate(
-            ((qn_hbm, qn), (qr_hbm, qr), (scale_hbm, scale), (table_hbm, table))
+            ((qn_hbm, qn), (qr_hbm, qr), (scale_hbm, scale), (table_hbm, table), (len_hbm, len_ref))
         )
     ]
     for copy in small:
@@ -185,6 +185,54 @@
     pair = jnp.concatenate([pair, jnp.zeros((LANES - rows, LANES), jnp.float32)], axis=0)
     stat[...] = pair.T[0:2]
 
+    n_dest = per_shard * n_head
+
+    @pl.when(own)
+    def _():
+        pl.semaphore_wait(barrier, n_dest - 1)
+
+    @pl.when(jnp.logical_not(own))
+    def _():
+        pl.semaphore_wait(barrier, n_dest)
+
+    def target(k):
+        part, request_of = k // n_head, k % n_head
+        slot = request_of * (heads // per_msg) + (part * width) // (vdim * per_msg)
+        return my_head * per_shard + part, request_of, slot
+
+    def remote(n, k):
+        seq_of, head_of, slot = target(k)
+        return pltpu.make_async_remote_copy(
+            src_ref=stat if n == 0 else msg.at[slot],
+            dst_ref=stat_in.at[my_seq] if n == 0 else acc_in.at[my_seq],
+            send_sem=send_sem.at[n, k],
+            recv_sem=recv_sem.at[n, my_seq],
+            device_id=(jnp.int32(seq_of), jnp.int32(head_of)),
+            device_id_type=MESH,
+        )
+
+    def local(n, i, slot):
+        return pltpu.make_async_copy(
+            stat if n == 0 else msg.at[slot],
+            stat_in.at[i] if n == 0 else acc_in.at[i],
+            recv_sem.at[n, i],
+        )
+
+    def is_me(k):
+        seq_of, head_of, _ = target(k)
+        return jnp.logical_and(seq_of == my_seq, head_of == my_head)
+
+    def send(n, k):
+        @pl.when(jnp.logical_not(is_me(k)))
+        def _():
+            remote(n, k).start()
+
+        @pl.when(is_me(k))
+        def _():
+            local(n, my_seq, target(k)[2]).start()
+
+    loop(n_dest, functools.partial(send, 0))
+
     high = acc.astype(jnp.bfloat16)
     low = (acc - high.astype(jnp.float32)).astype(jnp.bfloat16)
     both = jnp.concatenate([high, low], axis=0)
@@ -201,65 +249,9 @@
         carried = jnp.where(out_head == h + 1, y[:, vdim:], carried)
     msg[...] = carried.reshape(msg.shape)
 
-    n_dest = per_shard * n_head
-
-    @pl.when(own)
-    def _():
-        pl.semaphore_wait(barrier, n_dest - 1)
-
-    @pl.when(jnp.logical_not(own))
-    def _():
-        pl.semaphore_wait(barrier, n_dest)
-
-    def target(k):
-        part, request_of = k // n_head, k % n_head
-        slot = request_of * (heads // per_msg) + (part * width) // (vdim * per_msg)
-        return my_head * per_shard + part, request_of, slot
-
-    def pair_to(k):
-        seq_of, head_of, slot = target(k)
-        return [
-            pltpu.make_async_remote_copy(
-                src_ref=src, dst_ref=dst, send_sem=send_sem.at[n, k], recv_sem=recv_sem.at[n, my_seq],
-                device_id=(jnp.int32(seq_of), jnp.int32(head_of)), device_id_type=MESH,
-            )
-            for n, (src, dst) in enumerate(
-                ((stat, stat_in.at[my_seq]), (msg.at[slot], acc_in.at[my_seq]))
-            )
-        ]
-
-    def local_pair(k):
-        slot = target(k)[2]
-        return [
-            pltpu.make_async_copy(src, dst, recv_sem.at[n, my_seq])
-            for n, (src, dst) in enumerate(
-                ((stat, stat_in.at[my_seq]), (msg.at[slot], acc_in.at[my_seq]))
-            )
-        ]
-
-    def is_me(k):
-        seq_of, head_of, _ = target(k)
-        return jnp.logical_and(seq_of == my_seq, head_of == my_head)
-
-    def send(k):
-        @pl.when(jnp.logical_not(is_me(k)))
-        def _():
-            for copy in pair_to(k):
-                copy.start()
-
-        @pl.when(is_me(k))
-        def _():
-            for copy in local_pair(k):
-                copy.start()
-
-    loop(n_dest, send)
-
-    def receive(i):
-        for n, (src, dst) in enumerate(((stat, stat_in.at[i]), (msg.at[0], acc_in.at[i]))):
-            pltpu.make_async_copy(src, dst, recv_sem.at[n, i]).wait()
-
-    loop(n_seq, receive)
-
+    loop(n_dest, functools.partial(send, 1))
+
+    loop(n_seq, lambda i: local(0, i, 0).wait())
     peaks, totals = stat_in[:, 0, :], stat_in[:, 1, :]
     factor = jnp.exp(peaks - jnp.max(peaks, axis=0, keepdims=True))
     denominator = jnp.sum(factor * totals, axis=0, keepdims=True)
@@ -272,6 +264,7 @@
     mix[...] = factor.T.reshape(mix.shape)
     first = (my_seq % per_shard) * width
     weights = mix[my_head * (heads // per_msg) + first // (vdim * per_msg)]
+    loop(n_seq, lambda i: local(1, i, 0).wait())
     result = jnp.zeros((per_msg, vdim), jnp.float32)
     for i in range(n_seq):
         result = result + weights[:, i : i + 1] * acc_in[i]
@@ -288,8 +281,8 @@
     def sent(k):
         @pl.when(jnp.logical_not(is_me(k)))
         def _():
-            for copy in pair_to(k):
-                copy.wait_send()
+            for n in range(2):
+                remote(n, k).wait_send()
 
     loop(n_dest, sent)
 
@@ -310,17 +303,17 @@
         return pl.pallas_call(
             functools.partial(kernel, n_seq, n_head, width),
             out_shape=pltpu.VMEM((1, width), jnp.bfloat16),
-            in_specs=[pl.BlockSpec(memory_space=pl.ANY)] * 7
-            + [pl.BlockSpec(memory_space=pltpu.SMEM)],
+            in_specs=[pl.BlockSpec(memory_space=pl.ANY)] * 8,
             out_specs=pl.BlockSpec(memory_space=pltpu.VMEM),
             scratch_shapes=[vmem(a) for a in big]
             + [
+                pltpu.SMEM(lengths.shape, lengths.dtype),
                 pltpu.VMEM((batch * heads // per_msg, per_msg, vdim), jnp.float32),
                 pltpu.VMEM((2, LANES), jnp.float32),
                 pltpu.VMEM((n_seq, per_msg, vdim), jnp.float32),
                 pltpu.VMEM((n_seq, 2, LANES), jnp.float32),
                 pltpu.VMEM((LANES // per_msg, per_msg, LANES), jnp.float32),
-                pltpu.SemaphoreType.DMA((4,)),
+                pltpu.SemaphoreType.DMA((5,)),
                 pltpu.SemaphoreType.DMA((WK_PARTS,)),
                 pltpu.SemaphoreType.DMA((CHUNKS,)),
                 pltpu.SemaphoreType.DMA((WV_PARTS,)),

time: 15.7 us -> 14.7 us (0.936)
  Pallas kernels: 14.9 us -> 13.9 us
    pallas_call x1, Pallas kernels: 14.9 us -> 13.9 us  [shards(): pl.pallas_call(functools.partial(kernel, n_seq, n_head, width), out_shape...]
where the time goes in v3:
time: 14.7 us; the launch traced here: 14.5 us
  Pallas kernels  13.9 us (95%)
  local copies, waits for them, and re-layouts  0.6 us (4%)
    pallas_call x1, Pallas kernels, shards(): pl.pallas_call(functools.partial(kernel, n_seq, n_head, width), out_shape...  13.9 us
    unnamed x1, local copies, waits for them, and re-layouts  0.6 us

profile of v3, /device:TPU:0, one launch (start us, length us, event | category | flops | bytes accessed | tf_op | source)
XLA Modules:
  0.0 14.5 jit_solution(7686770167538551963)
XLA Ops:
  0.0 13.9 %shard_map.82 = bf16[1,1024]{1,0:T(2,128)(2,1)S(1)} custom-call(bf16[4,16,128]{2,1,0:T(8,128)(2,1)} %qn_hbm.1, bf16[4,16,64]{2,1,0:T(8,128)(2,1)} %qr_hbm.1, bf16[16,128,512]{2,1,0:T(8,128)(2,1)} %wk_hbm.1, bf16[16,512,128]{2,1,0:T(8,128)(2,1)} %wv_hbm.1, bf16[64,64,576]{2,1,0:T(8,128)(2,1)} %kv_hbm.1, f32[1,64]{1,0:T(1,128)} %bitcast.1, s32[4,16]{1,0:T(4,128)} %table_hbm.1, ...), custom_call_target="tpu_custom_call" | custom-call | tf_op jit(solution)/shard_map/pallas_call | solution.py:303
  13.9 0.6 %copy.10 = bf16[1,1024]{1,0:T(2,128)(2,1)} copy(bf16[1,1024]{1,0:T(2,128)(2,1)S(1)} %shard_map.82) | data formatting | bytes 4096

commit v4 on v3

--- a/solution.py
+++ b/solution.py
@@ -11,7 +11,7 @@
 floor_peak = -1e29
 LANES = 128
 CHUNKS = 4
-WV_PARTS = 2
+WV_PARTS = 1
 WINDOW = 6
 WK_PARTS = 4
 MESH = pl.DeviceIdType.MESH

time: 14.7 us -> 14.5 us (0.986)
  Pallas kernels: 13.9 us -> 13.7 us
    pallas_call x1, Pallas kernels: 13.9 us -> 13.7 us  [shards(): pl.pallas_call(functools.partial(kernel, n_seq, n_head, width), out_shape...]
where the time goes in v4:
time: 14.5 us; the launch traced here: 14.3 us
  Pallas kernels  13.7 us (94%)
  local copies, waits for them, and re-layouts  0.6 us (4%)
    pallas_call x1, Pallas kernels, shards(): pl.pallas_call(functools.partial(kernel, n_seq, n_head, width), out_shape...  13.7 us
    unnamed x1, local copies, waits for them, and re-layouts  0.6 us

profile of v4, /device:TPU:0, one launch (start us, length us, event | category | flops | bytes accessed | tf_op | source)
XLA Modules:
  0.0 14.3 jit_solution(1269902895066272675)
XLA Ops:
  0.0 13.7 %shard_map.82 = bf16[1,1024]{1,0:T(2,128)(2,1)S(1)} custom-call(bf16[4,16,128]{2,1,0:T(8,128)(2,1)} %qn_hbm.1, bf16[4,16,64]{2,1,0:T(8,128)(2,1)} %qr_hbm.1, bf16[16,128,512]{2,1,0:T(8,128)(2,1)} %wk_hbm.1, bf16[16,512,128]{2,1,0:T(8,128)(2,1)} %wv_hbm.1, bf16[64,64,576]{2,1,0:T(8,128)(2,1)} %kv_hbm.1, f32[1,64]{1,0:T(1,128)} %bitcast.1, s32[4,16]{1,0:T(4,128)} %table_hbm.1, ...), custom_call_target="tpu_custom_call" | custom-call | tf_op jit(solution)/shard_map/pallas_call | solution.py:303
  13.7 0.6 %copy.10 = bf16[1,1024]{1,0:T(2,128)(2,1)} copy(bf16[1,1024]{1,0:T(2,128)(2,1)S(1)} %shard_map.82) | data formatting | bytes 4096
